TPU v7x, 32 devices: a whole 2x2x4 slice. The times are simulated.
32 devices in a mesh: dp: 4 (over y, x), vocab: 8 (over z, core).
Axes of the slice: x: 2, y: 2, z: 4, core: 2. Of those that a mesh axis runs over, the one named last changes fastest.
Arguments:
- hidden: bfloat16 [2048, 5120], P(('dp', 'vocab')), may hold values from -100 to 100
- tokens: int32 [2048], P('dp'), may hold values from 0 to 9215
- old_weight: bfloat16 [9216, 5120], P('vocab'), may hold values from -1 to 1
- new_weight: bfloat16 [9216, 5120], P('dp', 'vocab'), may hold values from -6 to 6
Outputs:
- logprob: float32 [2048], P(('dp', 'vocab'))
- engine_weight: bfloat16 [9216, 5120], P('vocab')
All inputs are finite; a program needn't handle non-finite values.
Results may differ from a plain program's by a relative error of at most 0.001.
Values may be sent and summed in bfloat16 or wider, within the bound.
A program may use at most 128 MiB of HBM per device.

v0:
```python
import jax
import jax.numpy as jnp
from jax import lax
from jax.sharding import PartitionSpec as P


def combined_all(part, axis, combine):
    gathered = jax.tree.map(lambda a: lax.all_gather(a, axis), part)

    def take(source):
        return jax.tree.map(lambda a: lax.dynamic_index_in_dim(a, source, 0, False), gathered)

    return lax.fori_loop(
        1, lax.axis_size(axis), lambda source, state: combine(state, take(source)), take(0)
    )


def join_stats(earlier, later):
    high = jnp.maximum(earlier[0], later[0])
    summed = earlier[1] * jnp.exp(earlier[0] - high) + later[1] * jnp.exp(later[0] - high)
    return (high, summed, earlier[2] + later[2])


def on_device(hidden, tokens, old_weight, new_weight):
    ranks = lax.axis_size("vocab")
    rank = lax.axis_index("vocab")
    vocab_rows = old_weight.shape[0]
    first_id = rank * vocab_rows
    own_rows = hidden.shape[0]
    logits = lax.dot_general(
        lax.all_gather(hidden, "vocab", axis=0, tiled=True),
        old_weight,
        (((1,), (1,)), ((), ())),
        preferred_element_type=jnp.float32,
    )
    highest = jnp.max(logits, axis=1)
    summed = jnp.sum(jnp.exp(logits - highest[:, None]), axis=1)
    wanted = tokens - first_id
    columns = lax.broadcasted_iota(jnp.int32, logits.shape, 1)
    target = jnp.sum(jnp.where(columns == wanted[:, None], logits, 0.0), axis=1)
    stats = jnp.stack([highest, summed, target], axis=0)
    highest, summed, target = (stats[0], stats[1], stats[2])
    highest, summed, target = combined_all((highest, summed, target), "vocab", join_stats)
    row_first = rank * own_rows
    highest = lax.dynamic_slice_in_dim(highest, row_first, own_rows)
    summed = lax.dynamic_slice_in_dim(summed, row_first, own_rows)
    target = lax.dynamic_slice_in_dim(target, row_first, own_rows)
    logprob = target - highest - jnp.log(summed)
    replicas = lax.axis_size("dp")
    trainer_cols = new_weight.shape[1]
    owned = lax.all_to_all(
        lax.all_to_all(new_weight, "dp", split_axis=1, concat_axis=0, tiled=True),
        "vocab",
        split_axis=0,
        concat_axis=1,
        tiled=True,
    )
    owner_count = owned.shape[0]
    shaped_pieces = owned.reshape(owner_count, ranks, 1, trainer_cols // replicas)
    complete = lax.all_gather(shaped_pieces, "dp", axis=2, tiled=True)
    engine_weight = complete.reshape(owner_count, ranks * trainer_cols)
    return (logprob, engine_weight)


def solution(mesh):
    return jax.shard_map(
        on_device,
        mesh=mesh,
        in_specs=(P(("dp", "vocab"), None), P("dp"), P("vocab", None), P("dp", "vocab")),
        out_specs=(P(("dp", "vocab")), P("vocab", None)),
        check_vma=False,
    )
```

profile of v0, /device:TPU:0, one launch (start us, length us, event | category | flops | bytes accessed | tf_op | source)
XLA Modules:
  0.0 281.5 jit_solution(10585603467316577974)
XLA Ops:
  7.2 0.0 all-gather.10.cloned.1.call-start
  7.2 0.7 all-gather.10.cloned.1.call-update
  7.9 0.0 all-gather.12.cloned.1.call-start
  7.9 3.9 %copy.12 = bf16[2304,640]{0,1:T(8,128)(2,1)S(1)} copy(bf16[2304,640]{1,0:T(8,128)(2,1)} %param.9) | data formatting | bytes 5898240 | tf_op args[3]
  11.9 39.7 %all_to_all.32 = bf16[2304,4,160]{0,2,1:T(8,128)(2,1)S(1)} all-to-all(bf16[2304,4,160]{0,2,1:T(8,128)(2,1)S(1)} %bitcast.35), channel_id=1, replica_groups=mesh['dp'=4,'vocab'=8] {'dp'}, dimensions={1} | all-to-all | bytes 5898240 | tf_op jit(solution)/shard_map/all_to_all | solution.py:52
  51.6 2.3 copy.13
  53.8 2.9 %all_to_all.27 = bf16[8,1152,160]{1,0,2:T(8,128)(2,1)} reshape(bf16[4,2304,160]{1,0,2:T(4,128)(2,1)S(1)} %copy.13) | data formatting | bytes 5898240 | tf_op jit(solution)/shard_map/all_to_all | solution.py:51
  56.7 2.2 copy.14
  59.0 72.0 %all_to_all.33 = bf16[8,1152,160]{1,2,0:T(8,128)(2,1)S(1)} all-to-all(bf16[8,1152,160]{1,2,0:T(8,128)(2,1)S(1)} %copy.14), channel_id=1, replica_groups=mesh['dp'=4,'vocab'=8] {'vocab'}, dimensions={0} | all-to-all | bytes 5898240 | tf_op jit(solution)/shard_map/all_to_all | solution.py:51
  130.9 2.5 copy.15
  133.5 0.0 copy-start
  133.5 0.0 all-gather.12.cloned.1.call-update
  133.5 0.7 copy-done
  134.1 0.0 all-gather.10.cloned.1.call-done
  134.1 11.2 %fusion = (f32[512]{0:T(512)S(1)}, f32[512,1152]{1,0:T(8,128)S(1)}) fusion(bf16[512,5120]{1,0:T(8,128)(2,1)} %all-gather.10.cloned.1.call-done, bf16[1152,5120]{1,0:T(8,128)(2,1)} %param.8), kind=kOutput, calls=%fused_computation.12 | convolution fusion | flops 6040387072 | bytes 19400704 | tf_op jit(solution)/shard_map/dot_general | solution.py:30
  145.4 0.9 select_reduce_fusion
  146.3 12.8 %all-gather.5 = f32[8,1,512]{2,1,0:T(1,128)S(1)} all-gather(f32[1,1,512]{2,1,0:T(1,128)S(1)} %bitcast.47), channel_id=3, replica_groups=mesh['dp'=4,'vocab'=8] {'vocab'}, dimensions={0}, use_global_device_ids=true | all-gather | bytes 18432 | tf_op jit(solution)/shard_map/all_gather | solution.py:8
  159.1 12.8 %all-gather.6 = f32[8,1,512]{2,1,0:T(1,128)S(1)} all-gather(f32[1,1,512]{2,1,0:T(1,128)S(1)} %bitcast.46), channel_id=4, replica_groups=mesh['dp'=4,'vocab'=8] {'vocab'}, dimensions={0}, use_global_device_ids=true | all-gather | bytes 18432 | tf_op jit(solution)/shard_map/all_gather | solution.py:8
  171.8 12.8 %all-gather.4 = f32[8,1,512]{2,1,0:T(1,128)S(1)} all-gather(f32[1,1,512]{2,1,0:T(1,128)S(1)} %bitcast.45), channel_id=2, replica_groups=mesh['dp'=4,'vocab'=8] {'vocab'}, dimensions={0}, use_global_device_ids=true | all-gather | bytes 18432 | tf_op jit(solution)/shard_map/all_gather | solution.py:8
  184.6 0.6 while.19
  185.2 0.6 log_subtract_fusion
  185.8 61.4 %all-gather.12.cloned.1.call-done = bf16[1152,8,640]{0,1,2:T(8,128)(2,1)} async-done(((bf16[1152,8,160]{0,1,2:T(8,128)(2,1)}), bf16[1152,8,640]{0,1,2:T(8,128)(2,1)}) %all-gather.12.cloned.1.call-update) | async-done | bytes 11796496 | tf_op jit(solution)/shard_map/all_gather | solution.py:60
  247.2 11.2 %copy.16 = bf16[1152,8,640]{0,2,1:T(8,128)(2,1)} copy(bf16[1152,8,640]{0,1,2:T(8,128)(2,1)} %all-gather.12.cloned.1.call-done) | data formatting | bytes 23592960 | tf_op jit(solution)/shard_map/all_gather | solution.py:60
  258.4 16.3 %copy.17 = bf16[1152,5120]{1,0:T(8,128)(2,1)} copy(bf16[1152,5120]{0,1:T(8,128)(2,1)} %bitcast.32) | data formatting | bytes 23592960
  (35 shorter events, 0.4 us)
Async XLA Ops:
  7.2 127.0 %all-gather.10.cloned.1.call-start = ((), (), s32[]{:S(2)}) async-start(), calls=%async_computation.2 | async-start | bytes 5898240 | tf_op jit(solution)/shard_map/all_gather | solution.py:31
  7.9 239.3 %all-gather.12.cloned.1.call-start = ((), (), s32[]{:S(2)}) async-start(), calls=%async_computation.3 | async-start | bytes 14745600 | tf_op jit(solution)/shard_map/all_gather | solution.py:60
  133.5 0.7 copy-start
Sparse Core Ops, SparseCore 0:
  9.6 58.6 all-gather.9
  133.6 113.5 all-gather.11
where the time goes:
time: 282 us; the launch traced here: 281 us
  blocking collectives  150 us (53%)
  waiting for transfers between devices  62.1 us (22%)
  local copies, waits for them, and re-layouts  42.1 us (15%)
  between operations  14.1 us (5%)
  matrix products  11.2 us (4%)
    all_to_all x1, blocking collectives, on_device(): lax.all_to_all(lax.all_to_all(new_weight, 'dp', split_axis=1, concat_axis...  72 us
    all_gather x1, waiting for transfers between devices, on_device(): complete = lax.all_gather(shaped_pieces, 'dp', axis=2, tiled=True)  61.4 us
    all_to_all x1, blocking collectives, on_device(): lax.all_to_all(new_weight, 'dp', split_axis=1, concat_axis=0, tiled=True)  39.7 us
    all_gather x3, blocking collectives, combined_all(): gathered = jax.tree.map(lambda a: lax.all_gather(a, axis), part)  38.3 us
    unnamed x7, local copies, waits for them, and re-layouts  20.9 us
    dot_general x1, matrix products, on_device(): lax.dot_general(lax.all_gather(hidden, 'vocab', axis=0, tiled=True), old_...  11.2 us
    all_gather x1, local copies, waits for them, and re-layouts, on_device(): complete = lax.all_gather(shaped_pieces, 'dp', axis=2, tiled=True)  11.2 us
    all_to_all x3, local copies, waits for them, and re-layouts, on_device(): lax.all_to_all(lax.all_to_all(new_weight, 'dp', split_axis=1, concat_axis...  7.63 us
  transfers between devices with their start and end apart: 2, of which 1 were waited for; matrix products, arithmetic and copies ran while one was open for 9% of the time, Pallas kernels for 0%

commit v1 on v0

--- a/solution.py
+++ b/solution.py
@@ -47,18 +47,21 @@
     target = lax.dynamic_slice_in_dim(target, row_first, own_rows)
     logprob = target - highest - jnp.log(summed)
     replicas = lax.axis_size("dp")
-    trainer_cols = new_weight.shape[1]
-    owned = lax.all_to_all(
-        lax.all_to_all(new_weight, "dp", split_axis=1, concat_axis=0, tiled=True),
-        "vocab",
-        split_axis=0,
-        concat_axis=1,
-        tiled=True,
-    )
-    owner_count = owned.shape[0]
-    shaped_pieces = owned.reshape(owner_count, ranks, 1, trainer_cols // replicas)
-    complete = lax.all_gather(shaped_pieces, "dp", axis=2, tiled=True)
-    engine_weight = complete.reshape(owner_count, ranks * trainer_cols)
+    trainer_rows, trainer_cols = new_weight.shape
+    owners = ranks // replicas
+    piece = trainer_rows // (owners * replicas)
+    chunks = 2
+    part = piece // chunks
+    rows = new_weight.reshape(owners, replicas, chunks, part, trainer_cols)
+    gathered = []
+    for chunk in range(chunks):
+        mine = jnp.swapaxes(rows[:, :, chunk], 0, 1)
+        mine = lax.all_to_all(mine, "dp", split_axis=0, concat_axis=0, tiled=True)
+        mine = mine.reshape(ranks, part, trainer_cols)
+        mine = lax.all_to_all(mine, "vocab", split_axis=0, concat_axis=0, tiled=True)
+        gathered.append(lax.all_gather(mine, "dp", axis=0))
+    complete = jnp.stack(gathered, axis=1)
+    engine_weight = jnp.swapaxes(complete, 2, 3).reshape(vocab_rows, ranks * trainer_cols)
     return (logprob, engine_weight)
 
 

time: 282 us -> 268 us (0.950)
  blocking collectives: 150 us -> 201 us
  waiting for transfers between devices: 62.1 us -> 18.3 us
  local copies, waits for them, and re-layouts: 42.1 us -> 15.2 us
  other arithmetic: 1.71 us -> 7.73 us
    all_to_all x2 -> x4, blocking collectives: 112 us -> 163 us  [the longest x2 103 us: on_device(): lax.all_to_all(mine, 'vocab', split_axis=0, concat_axis=0, tiled=True)]
    all_gather x1 -> x2, waiting for transfers between devices: 61.4 us -> 17.5 us  [on_device(): gathered.append(lax.all_gather(mine, 'dp', axis=0))]
    unnamed x7 -> x6, local copies, waits for them, and re-layouts: 20.9 us -> 5.51 us
    all_gather x1 -> x0, local copies, waits for them, and re-layouts: 11.2 us -> none  [on_device(): complete = lax.all_gather(shaped_pieces, 'dp', axis=2, tiled=True)]
    all_to_all x4 -> x0, local copies, waits for them, and re-layouts: 9.91 us -> none  [the longest x3 7.63 us: on_device(): lax.all_to_all(lax.all_to_all(new_weight, 'dp', split_axis=1, concat_axis...]
    transpose x0 -> x4, local copies, waits for them, and re-layouts: none -> 9.52 us  [the longest x1 7.19 us: on_device(): jnp.swapaxes(complete, 2, 3).reshape(vocab_rows, ranks * trainer_cols)]
    transpose x0 -> x1, other arithmetic: none -> 6.02 us  [on_device(): jnp.swapaxes(complete, 2, 3).reshape(vocab_rows, ranks * trainer_cols)]
  transfers between devices with their start and end apart: 2 -> 3, of which waited for: 1 -> 1; matrix products, arithmetic and copies ran while one was open for 9% -> 6% of each run, Pallas kernels for 0% -> 0%
where the time goes in v1:
time: 268 us; the launch traced here: 267 us
  blocking collectives  201 us (75%)
  waiting for transfers between devices  18.3 us (7%)
  local copies, waits for them, and re-layouts  15.2 us (6%)
  between operations  13.8 us (5%)
  matrix products  10.8 us (4%)
  other arithmetic  7.73 us (3%)
    all_to_all x2, blocking collectives, on_device(): lax.all_to_all(mine, 'vocab', split_axis=0, concat_axis=0, tiled=True)  103 us
    all_to_all x2, blocking collectives, on_device(): mine = lax.all_to_all(mine, 'dp', split_axis=0, concat_axis=0, tiled=True)  59.7 us
    all_gather x3, blocking collectives, combined_all(): gathered = jax.tree.map(lambda a: lax.all_gather(a, axis), part)  38.3 us
    all_gather x2, waiting for transfers between devices, on_device(): gathered.append(lax.all_gather(mine, 'dp', axis=0))  17.5 us
    dot_general x1, matrix products, on_device(): lax.dot_general(lax.all_gather(hidden, 'vocab', axis=0, tiled=True), old_...  10.8 us
    transpose x1, local copies, waits for them, and re-layouts, on_device(): jnp.swapaxes(complete, 2, 3).reshape(vocab_rows, ranks * trainer_cols)  7.19 us
    transpose x1, other arithmetic, on_device(): jnp.swapaxes(complete, 2, 3).reshape(vocab_rows, ranks * trainer_cols)  6.02 us
    unnamed x6, local copies, waits for them, and re-layouts  5.51 us
  transfers between devices with their start and end apart: 3, of which 1 were waited for; matrix products, arithmetic and copies ran while one was open for 6% of the time, Pallas kernels for 0%

profile of v1, /device:TPU:0, one launch (start us, length us, event | category | flops | bytes accessed | tf_op | source)
XLA Modules:
  0.0 267.3 jit_solution(10110194304707341188)
XLA Ops:
  7.2 0.0 all-gather.12.cloned.1.call-start
  7.2 0.7 all-gather.12.cloned.1.call-update
  7.9 0.0 all-gather.14.cloned.1.call-start
  7.9 2.1 slice_bitcast_fusion.1
  10.0 0.1 copy.9
  10.2 24.0 %all_to_all.20 = bf16[4,2,144,640]{3,2,1,0:T(8,128)(2,1)S(1)} all-to-all(bf16[4,2,144,640]{3,2,1,0:T(8,128)(2,1)S(1)} %copy.9), channel_id=1, replica_groups=mesh['dp'=4,'vocab'=8] {'dp'}, dimensions={0} | all-to-all | bytes 2949120 | tf_op jit(solution)/shard_map/all_to_all | solution.py:59
  34.1 64.1 %all_to_all.21 = bf16[8,144,640]{2,1,0:T(8,128)(2,1)} all-to-all(bf16[8,144,640]{2,1,0:T(8,128)(2,1)S(1)} %bitcast.48), channel_id=1, replica_groups=mesh['dp'=4,'vocab'=8] {'vocab'}, dimensions={0} | all-to-all | bytes 2949120 | tf_op jit(solution)/shard_map/all_to_all | solution.py:61
  98.3 0.0 all-gather.14.cloned.1.call-update
  98.3 0.0 all-gather.16.cloned.1.call-start
  98.3 0.1 copy.10
  98.5 35.7 %all_to_all.22 = bf16[4,2,144,640]{3,2,1,0:T(8,128)(2,1)S(1)} all-to-all(bf16[4,2,144,640]{3,2,1,0:T(8,128)(2,1)S(1)} %copy.10), channel_id=1, replica_groups=mesh['dp'=4,'vocab'=8] {'dp'}, dimensions={0} | all-to-all | bytes 2949120 | tf_op jit(solution)/shard_map/all_to_all | solution.py:59
  134.2 0.0 copy-start
  134.2 39.0 %all_to_all.23 = bf16[8,144,640]{2,1,0:T(8,128)(2,1)} all-to-all(bf16[8,144,640]{2,1,0:T(8,128)(2,1)S(1)} %bitcast.49), channel_id=1, replica_groups=mesh['dp'=4,'vocab'=8] {'vocab'}, dimensions={0} | all-to-all | bytes 2949120 | tf_op jit(solution)/shard_map/all_to_all | solution.py:61
  173.2 0.0 all-gather.16.cloned.1.call-update
  173.2 0.0 copy-done
  173.2 0.0 all-gather.12.cloned.1.call-done
  173.2 10.8 %fusion = (f32[512]{0:T(512)S(1)}, f32[512,1152]{1,0:T(8,128)S(1)}) fusion(bf16[512,5120]{1,0:T(8,128)(2,1)} %all-gather.12.cloned.1.call-done, bf16[1152,5120]{1,0:T(8,128)(2,1)} %param.8), kind=kOutput, calls=%fused_computation.15 | convolution fusion | flops 6040387072 | bytes 19400704 | tf_op jit(solution)/shard_map/dot_general | solution.py:30
  184.1 0.9 select_reduce_fusion
  185.0 12.8 %all-gather.6 = f32[8,1,512]{2,1,0:T(1,128)S(1)} all-gather(f32[1,1,512]{2,1,0:T(1,128)S(1)} %bitcast.62), channel_id=3, replica_groups=mesh['dp'=4,'vocab'=8] {'vocab'}, dimensions={0}, use_global_device_ids=true | all-gather | bytes 18432 | tf_op jit(solution)/shard_map/all_gather | solution.py:8
  197.8 12.8 %all-gather.7 = f32[8,1,512]{2,1,0:T(1,128)S(1)} all-gather(f32[1,1,512]{2,1,0:T(1,128)S(1)} %bitcast.61), channel_id=4, replica_groups=mesh['dp'=4,'vocab'=8] {'vocab'}, dimensions={0}, use_global_device_ids=true | all-gather | bytes 18432 | tf_op jit(solution)/shard_map/all_gather | solution.py:8
  210.5 12.8 %all-gather.5 = f32[8,1,512]{2,1,0:T(1,128)S(1)} all-gather(f32[1,1,512]{2,1,0:T(1,128)S(1)} %bitcast.60), channel_id=2, replica_groups=mesh['dp'=4,'vocab'=8] {'vocab'}, dimensions={0}, use_global_device_ids=true | all-gather | bytes 18432 | tf_op jit(solution)/shard_map/all_gather | solution.py:8
  223.3 0.6 while.19
  223.9 0.6 log_subtract_fusion
  224.5 0.0 all-gather.14.cloned.1.call-done
  224.5 17.5 %all-gather.16.cloned.1.call-done = bf16[32,144,640]{2,1,0:T(8,128)(2,1)} async-done(((bf16[8,144,640]{2,1,0:T(8,128)(2,1)}), bf16[32,144,640]{2,1,0:T(8,128)(2,1)}) %all-gather.16.cloned.1.call-update) | async-done | bytes 5898256 | tf_op jit(solution)/shard_map/all_gather | solution.py:62
  242.0 6.0 %maximum_bitcast_fusion = bf16[4,2,144,8,640]{4,2,3,0,1:T(8,128)(2,1)S(1)} fusion(bf16[4,1,8,144,640]{4,3,2,0,1:T(8,128)(2,1)} %bitcast.47, bf16[4,1,8,144,640]{4,3,2,0,1:T(8,128)(2,1)} %bitcast.46), kind=kLoop, calls=%fused_computation.4 | loop fusion | flops 5898240 | bytes 23592960 | tf_op jit(solution)/shard_map/transpose | solution.py:64
  248.0 7.2 %copy.11 = bf16[4,2,144,8,640]{4,3,2,1,0:T(8,128)(2,1)S(1)} copy(bf16[4,2,144,8,640]{4,2,3,0,1:T(8,128)(2,1)S(1)} %maximum_bitcast_fusion) | data formatting | bytes 23592960 | tf_op jit(solution)/shard_map/transpose | solution.py:64
  255.2 5.5 %copy.15 = bf16[144,8,8,640]{3,1,2,0:T(8,128)(2,1)} copy(bf16[144,8,8,640]{3,2,1,0:T(8,128)(2,1)S(1)} %bitcast.44) | data formatting | bytes 23592960
  (35 shorter events, 0.4 us)
Async XLA Ops:
  7.2 166.1 %all-gather.12.cloned.1.call-start = ((), (), s32[]{:S(2)}) async-start(), calls=%async_computation.4 | async-start | bytes 5898240 | tf_op jit(solution)/shard_map/all_gather | solution.py:31
  7.9 216.6 %all-gather.14.cloned.1.call-start = ((), (), s32[]{:S(2)}) async-start(), calls=%async_computation.5 | async-start | bytes 7372800 | tf_op jit(solution)/shard_map/all_gather | solution.py:62
  98.3 143.7 %all-gather.16.cloned.1.call-start = ((), (), s32[]{:S(2)}) async-start(), calls=%async_computation.6 | async-start | bytes 7372800 | tf_op jit(solution)/shard_map/all_gather | solution.py:62
  134.2 39.0 %copy-start = (s32[512]{0:T(512)S(1)}, s32[512]{0:T(512)}, u32[]{:S(2)}) copy-start(s32[512]{0:T(512)} %param.7) | copy-start | bytes 6148
Sparse Core Ops, SparseCore 0:
  9.6 86.2 all-gather.11
  98.4 74.8 all-gather.13
  175.2 66.7 all-gather.15
